TPU v7x, 32 devices: a whole 2x2x4 slice. The times are simulated.
32 devices in a mesh: group: 2 (over y), cp: 8 (over z, x), hd: 2 (over core).
Axes of the slice: x: 2, y: 2, z: 4, core: 2. Of those that a mesh axis runs over, the one named last changes fastest.
Arguments:
- doc_lengths: int32 [8], P('group'), parts along dimension 0, may hold values from 1 to 384, 1024 in all
- queries: bfloat16 [2048, 4096], P(('group', 'cp'), 'hd'), parts along dimension 0, may hold values from -52 to 52
- key_states: bfloat16 [2048, 1024], P(('group', 'cp'), 'hd'), parts along dimension 0, may hold values from -4 to 4
- value_head_states: bfloat16 [2048, 1024], P(('group', 'cp'), 'hd'), parts along dimension 0, may hold values from -6 to 6
- out_grad: bfloat16 [2048, 4096], P(('group', 'cp'), 'hd'), parts along dimension 0, may hold values from -6 to 6
Outputs:
- attended: bfloat16 [2048, 4096], P(('group', 'cp'), 'hd'), parts along dimension 0
- grad_queries: bfloat16 [2048, 4096], P(('group', 'cp'), 'hd'), parts along dimension 0
- grad_keys: bfloat16 [2048, 1024], P(('group', 'cp'), 'hd'), parts along dimension 0
- grad_values: bfloat16 [2048, 1024], P(('group', 'cp'), 'hd'), parts along dimension 0
There are 2 independent parts, one for each index of `group`. A program takes and returns all parts, laid end to end along the dimension named above; each array names one. Nothing has to cross between parts.
Inputs may be any that keep to these rules, and one draw needn't show every extreme that they name: `doc_lengths`: documents lie end to end in token order; their lengths sum to 1024.
All inputs are finite; a program needn't handle non-finite values.
Results may differ from a plain program's by a relative error of at most 0.028.
Values may be sent and summed in bfloat16 or wider, within the bound.
A program may use at most 64 MiB of HBM per device.

v0:
```python
import math

import jax
import jax.numpy as jnp
from jax import lax
from jax.sharding import PartitionSpec as P

HEAD_SIZE = 128
REACH = 3


masked_score = -1e30


def from_behind(value, axis, by):
    peers = lax.axis_size(axis)
    pairs = [(i, i + by) for i in range(peers) if 0 <= i + by < peers]
    return lax.ppermute(value, axis, pairs)


def document_ids(doc_lengths, positions):
    ends = jnp.cumsum(doc_lengths)
    counted = jnp.sum((ends[None, :] <= positions[:, None]).astype(jnp.int32), axis=1)
    return jnp.where(positions < 0, jnp.int32(-1), counted)


def attend(queries, window, out_grad, allowed):
    tok_rows = queries.shape[0]
    window_rows = window.shape[1]
    head_kv = window.shape[2] // HEAD_SIZE
    group_size = queries.shape[1] // window.shape[2]
    score_scale = 1.0 / math.sqrt(HEAD_SIZE)
    query_heads = queries.reshape(tok_rows, head_kv, group_size, HEAD_SIZE)
    key_heads = window[0].reshape(window_rows, head_kv, HEAD_SIZE)
    value_heads = window[1].reshape(window_rows, head_kv, HEAD_SIZE)
    grad_heads = out_grad.reshape(tok_rows, head_kv, group_size, HEAD_SIZE)
    scores = (
        jnp.einsum("qhgd,khd->hgqk", query_heads, key_heads, preferred_element_type=jnp.float32)
        * score_scale
    )
    scores = jnp.where(allowed, scores, masked_score)
    row_max = jnp.max(scores, axis=-1, keepdims=True)
    weights_raw = jnp.exp(scores - row_max)
    probs = weights_raw / jnp.sum(weights_raw, axis=-1, keepdims=True)
    probs_low = probs.astype(jnp.bfloat16)
    attended = jnp.einsum(
        "hgqk,khd->qhgd", probs_low, value_heads, preferred_element_type=jnp.float32
    ).astype(jnp.bfloat16)
    delta = jnp.sum(
        grad_heads.astype(jnp.float32) * attended.astype(jnp.float32), axis=-1
    ).transpose(1, 2, 0)
    grad_value = jnp.einsum(
        "hgqk,qhgd->khd", probs_low, grad_heads, preferred_element_type=jnp.float32
    )
    grad_probs = jnp.einsum(
        "qhgd,khd->hgqk", grad_heads, value_heads, preferred_element_type=jnp.float32
    )
    grad_scores = (probs * (grad_probs - delta[..., None])).astype(jnp.bfloat16)
    grad_query = (
        jnp.einsum("hgqk,khd->qhgd", grad_scores, key_heads, preferred_element_type=jnp.float32)
        * score_scale
    ).astype(jnp.bfloat16)
    grad_key = (
        jnp.einsum("hgqk,qhgd->khd", grad_scores, query_heads, preferred_element_type=jnp.float32)
        * score_scale
    )
    return (
        attended.reshape(tok_rows, -1),
        grad_query.reshape(tok_rows, -1),
        grad_key.reshape(window_rows, -1),
        grad_value.reshape(window_rows, -1),
    )


def shards(doc_lengths, queries, key_states, value_head_states, out_grad):
    tok_rows = queries.shape[0]
    block_count = REACH + 1
    level_count = block_count.bit_length() - 1
    device_index = lax.axis_index("cp")
    key_value = jnp.stack([key_states, value_head_states])
    window = key_value
    for level_index in range(level_count):
        earlier = from_behind(window, "cp", window.shape[1] // tok_rows)
        window = jnp.concatenate([earlier, window], axis=1)
    query_pos = device_index * tok_rows + lax.iota(jnp.int32, tok_rows)
    key_pos = (device_index - REACH) * tok_rows + lax.iota(jnp.int32, block_count * tok_rows)
    query_ids = document_ids(doc_lengths, query_pos)
    key_ids = document_ids(doc_lengths, key_pos)
    allowed = (query_ids[:, None] == key_ids[None, :]) & (key_pos[None, :] <= query_pos[:, None])
    attended, grad_queries, grad_key, grad_value = attend(queries, window, out_grad, allowed)
    partials = jnp.stack([grad_key, grad_value])
    summed = partials
    for level_index in range(level_count):
        half_width = summed.shape[1] // 2
        later = from_behind(summed[:, :half_width], "cp", -(half_width // tok_rows))
        summed = summed[:, half_width:] + later
    grad_keys = summed[0].astype(jnp.bfloat16)
    grad_values = summed[1].astype(jnp.bfloat16)
    return (attended, grad_queries, grad_keys, grad_values)


def solution(mesh):
    return jax.shard_map(
        shards,
        mesh=mesh,
        in_specs=(
            P("group"),
            P(("group", "cp"), "hd"),
            P(("group", "cp"), "hd"),
            P(("group", "cp"), "hd"),
            P(("group", "cp"), "hd"),
        ),
        out_specs=(
            P(("group", "cp"), "hd"),
            P(("group", "cp"), "hd"),
            P(("group", "cp"), "hd"),
            P(("group", "cp"), "hd"),
        ),
        check_vma=False,
    )
```

profile of v0, /device:TPU:0, one launch (start us, length us, event | category | flops | bytes accessed | tf_op | source)
XLA Modules:
  0.0 83.1 jit_solution(13639317767490587939)
XLA Ops:
  0.6 1.1 %copy.40 = bf16[128,512]{0,1:T(8,128)(2,1)S(1)} copy(bf16[128,512]{1,0:T(8,128)(2,1)} %param.7) | data formatting | bytes 262144 | tf_op args[2]
  1.7 1.0 %copy.41 = bf16[128,512]{0,1:T(8,128)(2,1)S(1)} copy(bf16[128,512]{1,0:T(8,128)(2,1)} %param.8) | data formatting | bytes 262144 | tf_op args[3]
  2.8 4.9 %collective-permute-start = (bf16[2,128,512]{1,2,0:T(8,128)(2,1)S(1)}, bf16[2,128,512]{1,2,0:T(8,128)(2,1)S(1)}, u32[]{:S(2)}, u32[]{:S(2)}) collective-permute-start(bf16[2,128,512]{1,2,0:T(8,128)(2,1)S(1)} %pad_maximum_fusion.1), channel_id=1, source_target_pairs={{0,2},{2,4},{4,6},{6,8},{8,10},{10,12},{12,14},{1,3},{3,5},{5,7},{... | collective-permute-start | bytes 786440 | tf_op jit(solution)/shard_map/ppermute | solution.py:18
  7.7 0.8 reduce-window.8
  8.5 0.1 convert_reduce_fusion.1
  8.6 1.3 %copy.45 = bf16[128,2048]{0,1:T(8,128)(2,1)S(1)} copy(bf16[128,2048]{1,0:T(8,128)(2,1)} %param.9) | data formatting | bytes 1048576 | tf_op args[4]
  9.9 0.3 copy.71
  10.2 3.0 %collective-permute-done = bf16[2,128,512]{1,2,0:T(8,128)(2,1)S(1)} collective-permute-done((bf16[2,128,512]{1,2,0:T(8,128)(2,1)S(1)}, bf16[2,128,512]{1,2,0:T(8,128)(2,1)S(1)}, u32[]{:S(2)}, u32[]{:S(2)}) %collective-permute-start) | collective-permute-done | bytes 262176 | tf_op jit(solution)/shard_map/ppermute | solution.py:18
  13.3 5.4 %collective-permute-start.1 = (bf16[2,256,512]{1,2,0:T(8,128)(2,1)S(1)}, bf16[2,256,512]{1,2,0:T(8,128)(2,1)S(1)}, u32[]{:S(2)}, u32[]{:S(2)}) collective-permute-start(bf16[2,256,512]{1,2,0:T(8,128)(2,1)S(1)} %maximum_maximum_fusion.1), channel_id=1, source_target_pairs={{0,4},{2,6},{4,8},{6,10},{8,12},{10,14},{1,5},{3,7},{5,9},{7,11},{... | collective-permute-start | bytes 1572872 | tf_op jit(solution)/shard_map/ppermute | solution.py:18
  18.7 0.1 convert_reduce_fusion
  18.8 0.2 compare_and_fusion
  19.0 10.0 %collective-permute-done.1 = bf16[2,256,512]{1,2,0:T(8,128)(2,1)S(1)} collective-permute-done((bf16[2,256,512]{1,2,0:T(8,128)(2,1)S(1)}, bf16[2,256,512]{1,2,0:T(8,128)(2,1)S(1)}, u32[]{:S(2)}, u32[]{:S(2)}) %collective-permute-start.1) | collective-permute-done | bytes 524320 | tf_op jit(solution)/shard_map/ppermute | solution.py:18
  29.0 0.1 maximum_maximum_fusion
  29.2 3.5 %fusion.18 = (f32[4,4,128]{2,1,0:T(4,128)S(1)}, f32[4,4,128,512]{2,3,1,0:T(8,128)}) fusion(pred[128,512]{0,1:T(8,128)(4,1)S(1)} %compare_and_fusion, bf16[512,4,128,1]{0,2,3,1:T(8,128)(2,1)S(1)} %bitcast.90, bf16[128,4,4,128]{0,3,2,1:T(8,128)(2,1)S(1)} %bitcast.84), kind=kOutput, calls=%fused_computation.41 | convolution fusion | flops 272630272 | bytes 5316608 | tf_op jit(solution)/shard_map/sub | solution.py:43
  32.6 2.7 %fusion.7 = bf16[4,4,128,512]{2,3,1,0:T(8,128)(2,1)S(1)} fusion(f32[4,4,128,512]{2,3,1,0:T(8,128)} %get-tuple-element.21, f32[4,4,128]{2,1,0:T(4,128)S(1)} %get-tuple-element.20), kind=kLoop, calls=%fused_computation.13 | loop fusion | flops 2097152 | bytes 6299648 | tf_op jit(solution)/shard_map/convert_element_type | solution.py:45
  35.3 1.3 %multiply_reduce_fusion = (f32[128,4,4]{0,2,1:T(4,128)S(1)}, bf16[4,128,4,128]{3,1,2,0:T(8,128)(2,1)}) fusion(bf16[128,2048]{0,1:T(8,128)(2,1)S(1)} %copy.45, bf16[512,4,128,1]{0,2,3,1:T(8,128)(2,1)S(1)} %bitcast.87, bf16[4,4,128,512]{2,3,1,0:T(8,128)(2,1)S(1)} %fusion.7), kind=kOutput, calls=%fused_computation.23 | convolution fusion | flops 269744128 | bytes 3678208 | tf_op jit(solution)/shard_map/hgqk,khd->qhgd/dot_general | solution.py:46
  36.6 0.8 fusion.19
  37.4 0.3 copy.53
  37.8 3.1 %fusion.2 = bf16[4,4,128,512]{2,3,1,0:T(8,128)(2,1)S(1)} fusion(bf16[512,4,128,1]{0,2,3,1:T(8,128)(2,1)S(1)} %bitcast.88, bf16[128,4,4,128]{0,3,2,1:T(8,128)(2,1)S(1)} %bitcast.81, f32[4,4,128]{2,1,0:T(4,128)S(1)} %bitcast.98, f32[4,4,128,512]{2,3,1,0:T(8,128)} %get-tuple-element.21, f32[4,4,128]{2,1,0:T(4,128)S(1)} %get-tuple-element.20), kind=kOutput, calls=%fused_computation.3 | convolution fusion | flops 272629760 | bytes 7356416 | tf_op jit(solution)/shard_map/qhgd,khd->hgqk/dot_general | solution.py:55
  40.9 0.8 fusion.8
  41.7 0.5 copy-done
  42.2 0.3 copy.52
  42.7 1.4 %collective-permute-start.2 = (f32[2,256,512]{2,1,0:T(8,128)S(1)}, f32[2,256,512]{2,1,0:T(8,128)S(1)}, u32[]{:S(2)}, u32[]{:S(2)}) collective-permute-start(f32[2,256,512]{2,1,0:T(8,128)S(1)} %pad_maximum_fusion), channel_id=1, source_target_pairs={{4,0},{6,2},{8,4},{10,6},{12,8},{14,10},{5,1},{7,3},{9,5},{11,7},{... | collective-permute-start | bytes 3145736 | tf_op jit(solution)/shard_map/ppermute | solution.py:18
  44.1 24.5 %collective-permute-done.2 = f32[2,256,512]{2,1,0:T(8,128)S(1)} collective-permute-done((f32[2,256,512]{2,1,0:T(8,128)S(1)}, f32[2,256,512]{2,1,0:T(8,128)S(1)}, u32[]{:S(2)}, u32[]{:S(2)}) %collective-permute-start.2) | collective-permute-done | bytes 1048608 | tf_op jit(solution)/shard_map/ppermute | solution.py:18
  68.6 0.2 fusion.11
  68.9 1.4 %collective-permute-start.3 = (f32[2,128,512]{2,1,0:T(8,128)S(1)}, f32[2,128,512]{2,1,0:T(8,128)S(1)}, u32[]{:S(2)}, u32[]{:S(2)}) collective-permute-start(f32[2,128,512]{2,1,0:T(8,128)S(1)} %slice.39), channel_id=1, source_target_pairs={{2,0},{4,2},{6,4},{8,6},{10,8},{12,10},{14,12},{3,1},{5,3},{7,5},{... | collective-permute-start | bytes 1572872 | tf_op jit(solution)/shard_map/ppermute | solution.py:18
  70.4 0.5 fusion.9
  70.9 1.0 %copy.55 = bf16[128,2048]{1,0:T(8,128)(2,1)} copy(bf16[128,2048]{0,1:T(8,128)(2,1)S(1)} %bitcast.89) | data formatting | bytes 1048576
  71.9 1.0 %copy.54 = bf16[128,2048]{1,0:T(8,128)(2,1)} copy(bf16[128,2048]{0,1:T(8,128)(2,1)S(1)} %bitcast.86) | data formatting | bytes 1048576
  72.9 9.4 %collective-permute-done.3 = f32[2,128,512]{2,1,0:T(8,128)S(1)} collective-permute-done((f32[2,128,512]{2,1,0:T(8,128)S(1)}, f32[2,128,512]{2,1,0:T(8,128)S(1)}, u32[]{:S(2)}, u32[]{:S(2)}) %collective-permute-start.3) | collective-permute-done | bytes 524320 | tf_op jit(solution)/shard_map/ppermute | solution.py:18
  82.3 0.1 fusion.12
  82.4 0.7 slice_bitcast_fusion
  (24 shorter events, 0.3 us)
Async XLA Ops:
  0.6 9.3 %copy-start.7 = (bf16[128,2048]{1,0:T(8,128)(2,1)S(1)}, bf16[128,2048]{1,0:T(8,128)(2,1)}, u32[]{:S(2)}) copy-start(bf16[128,2048]{1,0:T(8,128)(2,1)} %param.6) | copy-start | bytes 1572868
  2.8 10.4 %collective-permute-start = (bf16[2,128,512]{1,2,0:T(8,128)(2,1)S(1)}, bf16[2,128,512]{1,2,0:T(8,128)(2,1)S(1)}, u32[]{:S(2)}, u32[]{:S(2)}) collective-permute-start(bf16[2,128,512]{1,2,0:T(8,128)(2,1)S(1)} %pad_maximum_fusion.1), channel_id=1, source_target_pairs={{0,2},{2,4},{4,6},{6,8},{8,10},{10,12},{12,14},{1,3},{3,5},{5,7},{... | collective-permute-start | bytes 786440 | tf_op jit(solution)/shard_map/ppermute | solution.py:18
  10.2 18.9 %copy-start.2 = (bf16[128,2048]{0,1:T(8,128)(2,1)}, bf16[128,2048]{0,1:T(8,128)(2,1)S(1)}, u32[]{:S(2)}) copy-start(bf16[128,2048]{0,1:T(8,128)(2,1)S(1)} %copy.71) | copy-start | bytes 1572868
  13.3 15.7 %collective-permute-start.1 = (bf16[2,256,512]{1,2,0:T(8,128)(2,1)S(1)}, bf16[2,256,512]{1,2,0:T(8,128)(2,1)S(1)}, u32[]{:S(2)}, u32[]{:S(2)}) collective-permute-start(bf16[2,256,512]{1,2,0:T(8,128)(2,1)S(1)} %maximum_maximum_fusion.1), channel_id=1, source_target_pairs={{0,4},{2,6},{4,8},{6,10},{8,12},{10,14},{1,5},{3,7},{5,9},{7,11},{... | collective-permute-start | bytes 1572872 | tf_op jit(solution)/shard_map/ppermute | solution.py:18
  29.1 3.5 %copy-start.5 = (bf16[1,512,512]{1,2,0:T(8,128)(2,1)}, bf16[1,512,512]{1,2,0:T(8,128)(2,1)S(1)}, u32[]{:S(2)}) copy-start(bf16[1,512,512]{1,2,0:T(8,128)(2,1)S(1)} %get-tuple-element.16) | copy-start | bytes 1572868
  37.8 3.1 %copy-start.3 = (bf16[128,2048]{0,1:T(8,128)(2,1)S(1)}, bf16[128,2048]{0,1:T(8,128)(2,1)}, u32[]{:S(2)}) copy-start(bf16[128,2048]{0,1:T(8,128)(2,1)} %copy-done.2) | copy-start | bytes 1572868
  40.9 1.4 %copy-start = (bf16[4,4,128,512]{2,3,1,0:T(8,128)(2,1)}, bf16[4,4,128,512]{2,3,1,0:T(8,128)(2,1)S(1)}, u32[]{:S(2)}) copy-start(bf16[4,4,128,512]{2,3,1,0:T(8,128)(2,1)S(1)} %fusion.2) | copy-start | bytes 6291460
  42.7 27.7 %copy-start.1 = (bf16[4,4,128,512]{2,3,1,0:T(8,128)(2,1)S(1)}, bf16[4,4,128,512]{2,3,1,0:T(8,128)(2,1)}, u32[]{:S(2)}) copy-start(bf16[4,4,128,512]{2,3,1,0:T(8,128)(2,1)} %copy-done) | copy-start | bytes 6291460
  42.7 27.7 %copy-start.6 = (bf16[1,512,512]{1,2,0:T(8,128)(2,1)S(1)}, bf16[1,512,512]{1,2,0:T(8,128)(2,1)}, u32[]{:S(2)}) copy-start(bf16[1,512,512]{1,2,0:T(8,128)(2,1)} %copy-done.5) | copy-start | bytes 1572868
  42.7 26.0 %collective-permute-start.2 = (f32[2,256,512]{2,1,0:T(8,128)S(1)}, f32[2,256,512]{2,1,0:T(8,128)S(1)}, u32[]{:S(2)}, u32[]{:S(2)}) collective-permute-start(f32[2,256,512]{2,1,0:T(8,128)S(1)} %pad_maximum_fusion), channel_id=1, source_target_pairs={{4,0},{6,2},{8,4},{10,6},{12,8},{14,10},{5,1},{7,3},{9,5},{11,7},{... | collective-permute-start | bytes 3145736 | tf_op jit(solution)/shard_map/ppermute | solution.py:18
  68.9 3.0 %copy-start.4 = (bf16[4,128,4,128]{3,1,2,0:T(8,128)(2,1)S(1)}, bf16[4,128,4,128]{3,1,2,0:T(8,128)(2,1)}, u32[]{:S(2)}) copy-start(bf16[4,128,4,128]{3,1,2,0:T(8,128)(2,1)} %get-tuple-element.23) | copy-start | bytes 1572868
  68.9 13.4 %collective-permute-start.3 = (f32[2,128,512]{2,1,0:T(8,128)S(1)}, f32[2,128,512]{2,1,0:T(8,128)S(1)}, u32[]{:S(2)}, u32[]{:S(2)}) collective-permute-start(f32[2,128,512]{2,1,0:T(8,128)S(1)} %slice.39), channel_id=1, source_target_pairs={{2,0},{4,2},{6,4},{8,6},{10,8},{12,10},{14,12},{3,1},{5,3},{7,5},{... | collective-permute-start | bytes 1572872 | tf_op jit(solution)/shard_map/ppermute | solution.py:18
where the time goes:
time: 83.5 us; the launch traced here: 83.1 us
  waiting for transfers between devices  46.9 us (56%)
  starting transfers between devices  13.1 us (16%)
  matrix products  9.95 us (12%)
  local copies, waits for them, and re-layouts  7.74 us (9%)
  other arithmetic  4.47 us (5%)
  between operations  0.93 us (1%)
    ppermute x4, waiting for transfers between devices, from_behind(): return lax.ppermute(value, axis, pairs)  46.9 us
    ppermute x4, starting transfers between devices, from_behind(): return lax.ppermute(value, axis, pairs)  13.1 us
    unnamed x21, local copies, waits for them, and re-layouts  5.98 us
    sub x1, matrix products, attend(): weights_raw = jnp.exp(scores - row_max)  3.46 us
    dot_general x1, matrix products, attend(): jnp.einsum('qhgd,khd->hgqk', grad_heads, value_heads, preferred_element_t...  3.09 us
    convert_element_type x1, other arithmetic, attend(): probs_low = probs.astype(jnp.bfloat16)  2.69 us
  transfers between devices with their start and end apart: 4, of which 4 were waited for; matrix products, arithmetic and copies ran while one was open for 6% of the time, Pallas kernels for 0%

commit v1 on v0

v1 whole, which is shorter than its diff:
```python
import functools
import math

import jax
import jax.numpy as jnp
from jax import lax
from jax.experimental import pallas as pl
from jax.experimental.pallas import tpu as pltpu
from jax.sharding import PartitionSpec as P

HEAD = 128
REACH = 3
MASKED = -1e30
MESH = pl.DeviceIdType.MESH
A, B, C, D = range(4)


def kernel(
    n, docs, doc_ref, q_hbm, k_hbm, v_hbm, do_hbm, o_hbm, gq_hbm, gk_hbm, gv_hbm,
    kv, qb, db, ob, gqb, own, mid, part, back, outkv, bias,
    kv_sem, q_sem, out_sem, gout_sem, fs_sem, fr_sem, bs_sem, br_sem,
):
    tok = q_hbm.shape[0]
    heads = k_hbm.shape[1] // HEAD
    group = q_hbm.shape[1] // k_hbm.shape[1]
    me = lax.axis_index("cp")
    odd = lax.rem(me, 2)
    is_odd = odd == 1
    is_even = odd == 0
    partner = me + 1 - 2 * odd
    diag = me - 1 + 2 * odd
    own_rows = pl.ds(REACH * tok, tok)

    def rows(dist):
        return pl.ds((REACH - dist) * tok, tok)

    def cols(h):
        return pl.ds(h * HEAD, HEAD)

    kv_loads = []
    for g in range(heads):
        kv_loads.append([
            pltpu.make_async_copy(src.at[:, cols(g)], kv.at[g, t, own_rows], kv_sem.at[g, t])
            for t, src in enumerate((k_hbm, v_hbm))
        ])
        for c in kv_loads[g]:
            c.start()
    q_loads = []
    for h in range(heads * group):
        q_loads.append([
            pltpu.make_async_copy(q_hbm.at[:, cols(h)], qb.at[h], q_sem.at[0, h]),
            pltpu.make_async_copy(do_hbm.at[:, cols(h)], db.at[h], q_sem.at[1, h]),
        ])
        for c in q_loads[h]:
            c.start()

    barrier = pltpu.get_barrier_semaphore()
    offsets = (-2, -1, 1, 2)
    for off in offsets:
        @pl.when((me + off >= 0) & (me + off < n))
        def _():
            pl.semaphore_signal(barrier, inc=1, device_id={"cp": me + off}, device_id_type=MESH)
    behind = jnp.minimum(me, 2)
    ahead = jnp.minimum(n - 1 - me, 2)
    pl.semaphore_wait(barrier, behind + ahead)

    def fwd(kind, g, src_rows, dst_rows, to):
        return pltpu.make_async_remote_copy(
            src_ref=kv.at[g, :, src_rows], dst_ref=kv.at[g, :, dst_rows],
            send_sem=fs_sem.at[kind, g], recv_sem=fr_sem.at[kind, g],
            device_id={"cp": to}, device_id_type=MESH,
        )

    def fwd_a(g):
        return fwd(A, g, own_rows, rows(1), partner)

    def fwd_b(g):
        return fwd(B, g, own_rows, rows(2), me + 2)

    def fwd_c_out(g):
        return fwd(C, g, rows(2), pl.ds(odd * 2 * tok, tok), partner)

    def fwd_c_in(g):
        return fwd(C, g, rows(2), pl.ds((1 - odd) * 2 * tok, tok), partner)

    def fwd_d(g):
        return fwd(D, g, rows(2), rows(3), diag)

    has_a_out = is_even
    has_a_in = is_odd
    has_b_out = me + 2 < n
    has_b_in = me >= 2
    has_c = me >= 2
    has_d_out = is_odd & (me >= 3) & (me + 1 < n)
    has_d_in = is_even & (me >= 4)

    for g in range(heads):
        for c in kv_loads[g]:
            c.wait()
        @pl.when(has_b_out)
        def _():
            fwd_b(g).start()
        @pl.when(has_a_out)
        def _():
            fwd_a(g).start()

    for dist in range(1, REACH + 1):
        @pl.when(me < dist)
        def _():
            kv[:, :, (REACH - dist) * tok:(REACH - dist + 1) * tok, :] = jnp.zeros(
                (heads, 2, tok, HEAD), kv.dtype)

    window = (REACH + 1) * tok
    key_pos = (me - REACH) * tok + lax.broadcasted_iota(jnp.int32, (window, tok), 0)
    query_pos = me * tok + lax.broadcasted_iota(jnp.int32, (window, tok), 1)

    end = jnp.int32(0)
    crossed = jnp.zeros((window, tok), jnp.int32)
    def count(d, carry):
        end, crossed = carry
        end = end + doc_ref[d]
        return end, crossed + jnp.where((key_pos < end) & (query_pos >= end), 1, 0)
    if docs <= 8:
        for d in range(docs):
            end, crossed = count(d, (end, crossed))
    else:
        end, crossed = lax.fori_loop(0, docs, count, (end, crossed))
    allowed = (crossed == 0) & (key_pos <= query_pos) & (key_pos >= 0)
    bias[...] = jnp.where(allowed, 0.0, MASKED)

    def relay(g):
        @pl.when(has_b_in)
        def _():
            fwd_b(g).wait_recv()
        @pl.when(has_d_out)
        def _():
            fwd_d(g).start()
        @pl.when(has_c)
        def _():
            fwd_c_out(g).start()

    def arrive(g):
        @pl.when(has_a_in)
        def _():
            fwd_a(g).wait_recv()
        @pl.when(has_c)
        def _():
            fwd_c_in(g).wait_recv()
        @pl.when(has_d_in)
        def _():
            fwd_d(g).wait_recv()

    def bwd(kind, g, src_rows, to):
        return pltpu.make_async_remote_copy(
            src_ref=part.at[g, :, src_rows], dst_ref=back.at[kind, g],
            send_sem=bs_sem.at[kind, g], recv_sem=br_sem.at[kind, g],
            device_id={"cp": to}, device_id_type=MESH,
        )

    def bwd_a(g):
        return bwd(A, g, rows(1), partner)

    def bwd_b(g):
        return bwd(B, g, rows(2), me - 2)

    def bwd_c(g):
        return bwd(C, g, pl.ds((1 - odd) * 2 * tok, tok), partner)

    def bwd_d(g):
        return bwd(D, g, rows(3), diag)

    score_scale = 1.0 / math.sqrt(HEAD)
    exp_scale = score_scale * math.log2(math.e)
    nt = (((1,), (1,)), ((), ()))
    step = 2 if group % 2 == 0 else 1
    width = step * tok

    out_copies = []

    def compute(g):
        keys = kv[g, 0]
        values = kv[g, 1]
        keys_t = keys.T
        values_t = values.T
        grad_k = jnp.zeros((window, HEAD), jnp.float32)
        grad_v = jnp.zeros((window, HEAD), jnp.float32)
        mask = jnp.concatenate([bias[...]] * step, axis=1)
        for s in range(group // step):
            h0 = g * group + s * step
            for h in range(h0, h0 + step):
                for c in q_loads[h]:
                    c.wait()
            qs = qb[h0:h0 + step].reshape(width, HEAD)
            ds = db[h0:h0 + step].reshape(width, HEAD)
            scores = lax.dot_general(keys, qs, nt, preferred_element_type=jnp.float32) + mask
            top = jnp.max(scores, axis=0, keepdims=True)
            raw = jnp.exp2((scores - top) * exp_scale)
            probs = raw * (1.0 / jnp.sum(raw, axis=0, keepdims=True))
            low = probs.astype(jnp.bfloat16)
            att_t = jnp.dot(values_t, low, preferred_element_type=jnp.float32)
            grad_p = lax.dot_general(values, ds, nt, preferred_element_type=jnp.float32)
            delta = jnp.sum(probs * grad_p, axis=0, keepdims=True)
            grad_s = (probs * (grad_p - delta)).astype(jnp.bfloat16)
            grad_v = grad_v + jnp.dot(low, ds, preferred_element_type=jnp.float32)
            grad_k = grad_k + jnp.dot(grad_s, qs, preferred_element_type=jnp.float32)
            gq_t = jnp.dot(keys_t, grad_s, preferred_element_type=jnp.float32) * score_scale
            for j in range(step):
                h = h0 + j
                ob[h] = att_t[:, j * tok:(j + 1) * tok].T.astype(ob.dtype)
                gqb[h] = gq_t[:, j * tok:(j + 1) * tok].T.astype(gqb.dtype)
                for t, (buf, dst) in enumerate(((ob, o_hbm), (gqb, gq_hbm))):
                    c = pltpu.make_async_copy(buf.at[h], dst.at[:, cols(h)], out_sem.at[t, h])
                    c.start()
                    out_copies.append(c)
        for t, grad in enumerate((grad_k * score_scale, grad_v)):
            part[g, t] = grad[:REACH * tok].astype(part.dtype)
            mid[g, t] = grad[tok:2 * tok]
            own[g, t] = grad[REACH * tok:]

    def give_back(g):
        @pl.when(has_d_in)
        def _():
            bwd_d(g).start()
        @pl.when(has_c)
        def _():
            bwd_c(g).start()
        @pl.when(has_a_in)
        def _():
            bwd_a(g).start()

    def collect(g):
        @pl.when(has_c)
        def _():
            bwd_c(g).wait_recv()
            mid[g] = mid[g] + back[C, g].astype(jnp.float32)
        @pl.when(has_d_out)
        def _():
            bwd_d(g).wait_recv()
            mid[g] = mid[g] + back[D, g].astype(jnp.float32)
        @pl.when(has_b_in)
        def _():
            part[g, :, tok:2 * tok] = mid[g].astype(part.dtype)
            bwd_b(g).start()

    def finish(g):
        @pl.when(has_a_out)
        def _():
            bwd_a(g).wait_recv()
            own[g] = own[g] + back[A, g].astype(jnp.float32)
        @pl.when(has_b_out)
        def _():
            bwd_b(g).wait_recv()
            own[g] = own[g] + back[B, g].astype(jnp.float32)
        outkv[g] = own[g].astype(outkv.dtype)
        for t, dst in enumerate((gk_hbm, gv_hbm)):
            c = pltpu.make_async_copy(outkv.at[g, t], dst.at[:, cols(g)], gout_sem.at[t, g])
            c.start()
            out_copies.append(c)

    relay(0)
    for g in range(heads):
        if g + 1 < heads:
            relay(g + 1)
        arrive(g)
        compute(g)
        give_back(g)
        if g >= 1:
            collect(g - 1)
        if g >= 2:
            finish(g - 2)
    collect(heads - 1)
    for g in range(max(heads - 2, 0), heads):
        finish(g)

    for g in range(heads):
        for cond, copies in (
            (has_a_out, (fwd_a,)), (has_b_out, (fwd_b,)), (has_c, (fwd_c_out, bwd_c)),
            (has_d_out, (fwd_d,)), (has_a_in, (bwd_a,)), (has_b_in, (bwd_b,)), (has_d_in, (bwd_d,)),
        ):
            @pl.when(cond)
            def _():
                for f in copies:
                    f(g).wait_send()
    for c in out_copies:
        c.wait()


def shards(doc_lengths, queries, key_states, value_head_states, out_grad):
    tok = queries.shape[0]
    heads = key_states.shape[1] // HEAD
    q_heads = queries.shape[1] // HEAD
    n = lax.axis_size("cp")
    window = (REACH + 1) * tok
    bf16, f32 = jnp.bfloat16, jnp.float32
    any_spec = pl.BlockSpec(memory_space=pl.ANY)
    dma = pltpu.SemaphoreType.DMA
    return tuple(pl.pallas_call(
        functools.partial(kernel, n, doc_lengths.shape[0]),
        out_shape=[
            jax.ShapeDtypeStruct(queries.shape, bf16),
            jax.ShapeDtypeStruct(queries.shape, bf16),
            jax.ShapeDtypeStruct(key_states.shape, bf16),
            jax.ShapeDtypeStruct(key_states.shape, bf16),
        ],
        in_specs=[pl.BlockSpec(memory_space=pltpu.SMEM)] + [any_spec] * 4,
        out_specs=[any_spec] * 4,
        scratch_shapes=[
            pltpu.VMEM((heads, 2, window, HEAD), bf16),
            pltpu.VMEM((q_heads, tok, HEAD), bf16),
            pltpu.VMEM((q_heads, tok, HEAD), bf16),
            pltpu.VMEM((q_heads, tok, HEAD), bf16),
            pltpu.VMEM((q_heads, tok, HEAD), bf16),
            pltpu.VMEM((heads, 2, tok, HEAD), f32),
            pltpu.VMEM((heads, 2, tok, HEAD), f32),
            pltpu.VMEM((heads, 2, REACH * tok, HEAD), bf16),
            pltpu.VMEM((4, heads, 2, tok, HEAD), bf16),
            pltpu.VMEM((heads, 2, tok, HEAD), bf16),
            pltpu.VMEM((window, tok), f32),
            dma((heads, 2)),
            dma((2, q_heads)),
            dma((2, q_heads)),
            dma((2, heads)),
            dma((4, heads)),
            dma((4, heads)),
            dma((4, heads)),
            dma((4, heads)),
        ],
        compiler_params=pltpu.CompilerParams(
            collective_id=0, has_side_effects=True, vmem_limit_bytes=48 * 2**20),
        name="attend",
    )(doc_lengths, queries, key_states, value_head_states, out_grad))


def solution(mesh):
    wide = P(("group", "cp"), "hd")
    return jax.shard_map(
        shards,
        mesh=mesh,
        in_specs=(P("group"), wide, wide, wide, wide),
        out_specs=(wide, wide, wide, wide),
        check_vma=False,
    )
```

time: 83.5 us -> 47.7 us (0.57)
  waiting for transfers between devices: 46.9 us -> 0 us
  Pallas kernels: 0 us -> 38.8 us
  starting transfers between devices: 13.1 us -> 0 us
  matrix products: 9.95 us -> 0 us
  other arithmetic: 4.47 us -> 0 us
    ppermute x4 -> x0, waiting for transfers between devices: 46.9 us -> none  [from_behind(): return lax.ppermute(value, axis, pairs)]
    pallas_call x0 -> x1, Pallas kernels: none -> 38.8 us  [shards(): pl.pallas_call(functools.partial(kernel, n, doc_lengths.shape[0]), out_sh...]
    ppermute x4 -> x0, starting transfers between devices: 13.1 us -> none  [from_behind(): return lax.ppermute(value, axis, pairs)]
    dot_general x5 -> x0, matrix products: 6.5 us -> none  [the longest x1 3.09 us: attend(): jnp.einsum('qhgd,khd->hgqk', grad_heads, value_heads, preferred_element_t...]
    sub x1 -> x0, matrix products: 3.46 us -> none  [attend(): weights_raw = jnp.exp(scores - row_max)]
    convert_element_type x1 -> x0, other arithmetic: 2.69 us -> none  [attend(): probs_low = probs.astype(jnp.bfloat16)]
    unnamed x21 -> x14, local copies, waits for them, and re-layouts: 5.98 us -> 7.44 us
    another operation x4 -> x0, other arithmetic: 1.02 us -> none
  transfers between devices with their start and end apart: 4 -> 0, of which waited for: 4 -> 0; matrix products, arithmetic and copies ran while one was open for 6% -> 0% of each run, Pallas kernels for 0% -> 0%
where the time goes in v1:
time: 47.7 us; the launch traced here: 46.9 us
  Pallas kernels  38.8 us (81%)
  local copies, waits for them, and re-layouts  7.44 us (16%)
  between operations  0.65 us (1%)
    pallas_call x1, Pallas kernels, shards(): pl.pallas_call(functools.partial(kernel, n, doc_lengths.shape[0]), out_sh...  38.8 us
    unnamed x14, local copies, waits for them, and re-layouts  7.44 us

profile of v1, /device:TPU:0, one launch (start us, length us, event | category | flops | bytes accessed | tf_op | source)
XLA Modules:
  0.0 46.9 jit_solution(16326714458819519298)
XLA Ops:
  0.6 0.0 copy-start
  0.6 1.0 %copy-done = bf16[128,2048]{1,0:T(8,128)(2,1)S(1)} copy-done((bf16[128,2048]{1,0:T(8,128)(2,1)S(1)}, bf16[128,2048]{1,0:T(8,128)(2,1)}, u32[]{:S(2)}) %copy-start) | copy-done | bytes 524312
  1.7 0.0 copy-start.1
  1.7 1.0 %copy-done.1 = bf16[128,2048]{1,0:T(8,128)(2,1)S(1)} copy-done((bf16[128,2048]{1,0:T(8,128)(2,1)S(1)}, bf16[128,2048]{1,0:T(8,128)(2,1)}, u32[]{:S(2)}) %copy-start.1) | copy-done | bytes 524312
  2.7 0.0 copy-start.2
  2.7 0.9 %copy-done.2 = bf16[128,512]{1,0:T(8,128)(2,1)S(1)} copy-done((bf16[128,512]{1,0:T(8,128)(2,1)S(1)}, bf16[128,512]{1,0:T(8,128)(2,1)}, u32[]{:S(2)}) %copy-start.2) | copy-done | bytes 131096
  3.6 0.0 copy-start.3
  3.6 0.9 %copy-done.3 = bf16[128,512]{1,0:T(8,128)(2,1)S(1)} copy-done((bf16[128,512]{1,0:T(8,128)(2,1)S(1)}, bf16[128,512]{1,0:T(8,128)(2,1)}, u32[]{:S(2)}) %copy-start.3) | copy-done | bytes 131096
  4.5 0.0 copy-start.4
  4.5 0.7 %copy-done.4 = s32[4]{0:T(128)S(1)} copy-done((s32[4]{0:T(128)S(1)}, s32[4]{0:T(128)}, u32[]{:S(2)}) %copy-start.4) | copy-done | bytes 40
  5.2 38.8 %attend.1 = (bf16[128,2048]{1,0:T(8,128)(2,1)S(1)}, bf16[128,2048]{1,0:T(8,128)(2,1)S(1)}, bf16[128,512]{1,0:T(8,128)(2,1)S(1)}, bf16[128,512]{1,0:T(8,128)(2,1)S(1)}) custom-call(s32[4]{0:T(128)S(1)} %copy-done.4, bf16[128,2048]{1,0:T(8,128)(2,1)S(1)} %copy-done, bf16[128,512]{1,0:T(8,128)(2,1)S(1)} %copy-done.2, bf16[128,512]{1,0:T(8,128)(2,1)S(1)} %copy-done.3, ...), custom_call_target="tpu_custom_call" | custom-call | tf_op jit(solution)/shard_map/attend/pallas_call | solution.py:297
  44.0 0.8 %copy.13 = bf16[128,2048]{1,0:T(8,128)(2,1)} copy(bf16[128,2048]{1,0:T(8,128)(2,1)S(1)} %get-tuple-element.8) | data formatting | bytes 1048576
  44.8 0.8 %copy.14 = bf16[128,2048]{1,0:T(8,128)(2,1)} copy(bf16[128,2048]{1,0:T(8,128)(2,1)S(1)} %get-tuple-element.9) | data formatting | bytes 1048576
  45.6 0.7 %copy.15 = bf16[128,512]{1,0:T(8,128)(2,1)} copy(bf16[128,512]{1,0:T(8,128)(2,1)S(1)} %get-tuple-element.10) | data formatting | bytes 262144
  46.3 0.7 %copy.16 = bf16[128,512]{1,0:T(8,128)(2,1)} copy(bf16[128,512]{1,0:T(8,128)(2,1)S(1)} %get-tuple-element.11) | data formatting | bytes 262144
Async XLA Ops:
  0.6 1.0 %copy-start = (bf16[128,2048]{1,0:T(8,128)(2,1)S(1)}, bf16[128,2048]{1,0:T(8,128)(2,1)}, u32[]{:S(2)}) copy-start(bf16[128,2048]{1,0:T(8,128)(2,1)} %q_hbm.1) | copy-start | bytes 1572868
  1.7 1.0 %copy-start.1 = (bf16[128,2048]{1,0:T(8,128)(2,1)S(1)}, bf16[128,2048]{1,0:T(8,128)(2,1)}, u32[]{:S(2)}) copy-start(bf16[128,2048]{1,0:T(8,128)(2,1)} %do_hbm.1) | copy-start | bytes 1572868
  2.7 0.9 %copy-start.2 = (bf16[128,512]{1,0:T(8,128)(2,1)S(1)}, bf16[128,512]{1,0:T(8,128)(2,1)}, u32[]{:S(2)}) copy-start(bf16[128,512]{1,0:T(8,128)(2,1)} %k_hbm.1) | copy-start | bytes 393220
  3.6 0.9 %copy-start.3 = (bf16[128,512]{1,0:T(8,128)(2,1)S(1)}, bf16[128,512]{1,0:T(8,128)(2,1)}, u32[]{:S(2)}) copy-start(bf16[128,512]{1,0:T(8,128)(2,1)} %v_hbm.1) | copy-start | bytes 393220
  4.5 0.7 %copy-start.4 = (s32[4]{0:T(128)S(1)}, s32[4]{0:T(128)}, u32[]{:S(2)}) copy-start(s32[4]{0:T(128)} %doc_ref.1) | copy-start | bytes 52

commit v2 on v1

--- a/solution.py
+++ b/solution.py
@@ -16,9 +16,9 @@
 
 
 def kernel(
-    n, docs, doc_ref, q_hbm, k_hbm, v_hbm, do_hbm, o_hbm, gq_hbm, gk_hbm, gv_hbm,
-    kv, qb, db, ob, gqb, own, mid, part, back, outkv, bias,
-    kv_sem, q_sem, out_sem, gout_sem, fs_sem, fr_sem, bs_sem, br_sem,
+    n, docs, doc_hbm, q_hbm, k_hbm, v_hbm, do_hbm, o_ref, gq_ref, gk_ref, gv_ref,
+    kv, qb, db, own, mid, part, back, bias, doc_ref,
+    doc_sem, kv_sem, q_sem, fs_sem, fr_sem, bs_sem, br_sem,
 ):
     tok = q_hbm.shape[0]
     heads = k_hbm.shape[1] // HEAD
@@ -37,6 +37,8 @@
     def cols(h):
         return pl.ds(h * HEAD, HEAD)
 
+    doc_load = pltpu.make_async_copy(doc_hbm, doc_ref, doc_sem)
+    doc_load.start()
     kv_loads = []
     for g in range(heads):
         kv_loads.append([
@@ -114,6 +116,7 @@
     key_pos = (me - REACH) * tok + lax.broadcasted_iota(jnp.int32, (window, tok), 0)
     query_pos = me * tok + lax.broadcasted_iota(jnp.int32, (window, tok), 1)
 
+    doc_load.wait()
     end = jnp.int32(0)
     crossed = jnp.zeros((window, tok), jnp.int32)
     def count(d, carry):
@@ -174,8 +177,6 @@
     nt = (((1,), (1,)), ((), ()))
     step = 2 if group % 2 == 0 else 1
     width = step * tok
-
-    out_copies = []
 
     def compute(g):
         keys = kv[g, 0]
@@ -206,12 +207,8 @@
             gq_t = jnp.dot(keys_t, grad_s, preferred_element_type=jnp.float32) * score_scale
             for j in range(step):
                 h = h0 + j
-                ob[h] = att_t[:, j * tok:(j + 1) * tok].T.astype(ob.dtype)
-                gqb[h] = gq_t[:, j * tok:(j + 1) * tok].T.astype(gqb.dtype)
-                for t, (buf, dst) in enumerate(((ob, o_hbm), (gqb, gq_hbm))):
-                    c = pltpu.make_async_copy(buf.at[h], dst.at[:, cols(h)], out_sem.at[t, h])
-                    c.start()
-                    out_copies.append(c)
+                o_ref[:, cols(h)] = att_t[:, j * tok:(j + 1) * tok].T.astype(o_ref.dtype)
+                gq_ref[:, cols(h)] = gq_t[:, j * tok:(j + 1) * tok].T.astype(gq_ref.dtype)
         for t, grad in enumerate((grad_k * score_scale, grad_v)):
             part[g, t] = grad[:REACH * tok].astype(part.dtype)
             mid[g, t] = grad[tok:2 * tok]
@@ -251,11 +248,8 @@
         def _():
             bwd_b(g).wait_recv()
             own[g] = own[g] + back[B, g].astype(jnp.float32)
-        outkv[g] = own[g].astype(outkv.dtype)
-        for t, dst in enumerate((gk_hbm, gv_hbm)):
-            c = pltpu.make_async_copy(outkv.at[g, t], dst.at[:, cols(g)], gout_sem.at[t, g])
-            c.start()
-            out_copies.append(c)
+        gk_ref[:, cols(g)] = own[g, 0].astype(gk_ref.dtype)
+        gv_ref[:, cols(g)] = own[g, 1].astype(gv_ref.dtype)
 
     relay(0)
     for g in range(heads):
@@ -281,7 +275,16 @@
             def _():
                 for f in copies:
                     f(g).wait_send()
-    for c in out_copies:
+
+
+def put_out(*refs):
+    sems = refs[-1]
+    copies = [
+        pltpu.make_async_copy(refs[t], refs[4 + t], sems.at[t]) for t in range(4)
+    ]
+    for c in copies:
+        c.start()
+    for c in copies:
         c.wait()
 
 
@@ -292,9 +295,14 @@
     n = lax.axis_size("cp")
     window = (REACH + 1) * tok
     bf16, f32 = jnp.bfloat16, jnp.float32
+    hbm_spec = pl.BlockSpec(memory_space=pltpu.HBM)
     any_spec = pl.BlockSpec(memory_space=pl.ANY)
     dma = pltpu.SemaphoreType.DMA
-    return tuple(pl.pallas_call(
+    args = [
+        pltpu.with_memory_space_constraint(x, pltpu.HBM)
+        for x in (doc_lengths, queries, key_states, value_head_states, out_grad)
+    ]
+    outs = pl.pallas_call(
         functools.partial(kernel, n, doc_lengths.shape[0]),
         out_shape=[
             jax.ShapeDtypeStruct(queries.shape, bf16),
@@ -302,33 +310,39 @@
             jax.ShapeDtypeStruct(key_states.shape, bf16),
             jax.ShapeDtypeStruct(key_states.shape, bf16),
         ],
-        in_specs=[pl.BlockSpec(memory_space=pltpu.SMEM)] + [any_spec] * 4,
-        out_specs=[any_spec] * 4,
+        in_specs=[hbm_spec] * 5,
+        out_specs=[pl.BlockSpec(memory_space=pltpu.VMEM)] * 4,
         scratch_shapes=[
             pltpu.VMEM((heads, 2, window, HEAD), bf16),
-            pltpu.VMEM((q_heads, tok, HEAD), bf16),
-            pltpu.VMEM((q_heads, tok, HEAD), bf16),
             pltpu.VMEM((q_heads, tok, HEAD), bf16),
             pltpu.VMEM((q_heads, tok, HEAD), bf16),
             pltpu.VMEM((heads, 2, tok, HEAD), f32),
             pltpu.VMEM((heads, 2, tok, HEAD), f32),
             pltpu.VMEM((heads, 2, REACH * tok, HEAD), bf16),
             pltpu.VMEM((4, heads, 2, tok, HEAD), bf16),
-            pltpu.VMEM((heads, 2, tok, HEAD), bf16),
             pltpu.VMEM((window, tok), f32),
+            pltpu.SMEM(doc_lengths.shape, jnp.int32),
+            dma(()),
             dma((heads, 2)),
             dma((2, q_heads)),
-            dma((2, q_heads)),
-            dma((2, heads)),
             dma((4, heads)),
             dma((4, heads)),
             dma((4, heads)),
             dma((4, heads)),
         ],
         compiler_params=pltpu.CompilerParams(
-            collective_id=0, has_side_effects=True, vmem_limit_bytes=48 * 2**20),
+            collective_id=0, has_side_effects=True, vmem_limit_bytes=24 * 2**20),
         name="attend",
-    )(doc_lengths, queries, key_states, value_head_states, out_grad))
+    )(*args)
+    return tuple(pl.pallas_call(
+        put_out,
+        out_shape=[jax.ShapeDtypeStruct(x.shape, x.dtype) for x in outs],
+        in_specs=[any_spec] * 4,
+        out_specs=[hbm_spec] * 4,
+        scratch_shapes=[dma((4,))],
+        compiler_params=pltpu.CompilerParams(vmem_limit_bytes=2**20),
+        name="put_out",
+    )(*outs))
 
 
 def solution(mesh):

time: 47.7 us -> 39.4 us (0.83)
  local copies, waits for them, and re-layouts: 7.44 us -> 0 us
  Pallas kernels: 38.8 us -> 38 us
    unnamed x14 -> x0, local copies, waits for them, and re-layouts: 7.44 us -> none
    pallas_call x1, Pallas kernels: 38.8 us -> 36.9 us  [shards(): pl.pallas_call(functools.partial(kernel, n, doc_lengths.shape[0]), out_sh...]
    pallas_call x0 -> x1, Pallas kernels: none -> 1.08 us  [shards(): pl.pallas_call(put_out, out_shape=[jax.ShapeDtypeStruct(x.shape, x.dtype)...]
where the time goes in v2:
time: 39.4 us; the launch traced here: 38.7 us
  Pallas kernels  38 us (96%)
  between operations  0.64 us (2%)
    pallas_call x1, Pallas kernels, shards(): pl.pallas_call(functools.partial(kernel, n, doc_lengths.shape[0]), out_sh...  36.9 us
    pallas_call x1, Pallas kernels, shards(): pl.pallas_call(put_out, out_shape=[jax.ShapeDtypeStruct(x.shape, x.dtype)...  1.08 us

profile of v2, /device:TPU:0, one launch (start us, length us, event | category | flops | bytes accessed | tf_op | source)
XLA Modules:
  0.0 38.7 jit_solution(15842697169145424854)
XLA Ops:
  0.6 36.9 %attend.1 = (bf16[128,2048]{1,0:T(8,128)(2,1)S(1)}, bf16[128,2048]{1,0:T(8,128)(2,1)S(1)}, bf16[128,512]{1,0:T(8,128)(2,1)S(1)}, bf16[128,512]{1,0:T(8,128)(2,1)S(1)}) custom-call(s32[4]{0:T(128)} %doc_hbm.1, bf16[128,2048]{1,0:T(8,128)(2,1)} %q_hbm.1, bf16[128,512]{1,0:T(8,128)(2,1)} %k_hbm.1, bf16[128,512]{1,0:T(8,128)(2,1)} %v_hbm.1, bf16[128,2048]{1,0:T(8,128)(2,1)} %do_hbm.1), custom_call_target="tpu_custom_call" | custom-call | tf_op jit(solution)/shard_map/attend/pallas_call | solution.py:305
  37.6 1.1 %put_out.1 = (bf16[128,2048]{1,0:T(8,128)(2,1)}, bf16[128,2048]{1,0:T(8,128)(2,1)}, bf16[128,512]{1,0:T(8,128)(2,1)}, bf16[128,512]{1,0:T(8,128)(2,1)}) custom-call(bf16[128,2048]{1,0:T(8,128)(2,1)S(1)} %get-tuple-element.8.refs_0_, bf16[128,2048]{1,0:T(8,128)(2,1)S(1)} %get-tuple-element.9.refs_1_, bf16[128,512]{1,0:T(8,128)(2,1)S(1)} %get-tuple-element.10.refs_2_, ...), custom_call_target="tpu_custom_call" | custom-call | tf_op jit(solution)/shard_map/put_out/pallas_call | solution.py:337

commit v3 on v2

--- a/solution.py
+++ b/solution.py
@@ -12,7 +12,7 @@
 REACH = 3
 MASKED = -1e30
 MESH = pl.DeviceIdType.MESH
-A, B, C, D = range(4)
+X, B, T = range(3)
 
 
 def kernel(
@@ -28,7 +28,6 @@
     is_odd = odd == 1
     is_even = odd == 0
     partner = me + 1 - 2 * odd
-    diag = me - 1 + 2 * odd
     own_rows = pl.ds(REACH * tok, tok)
 
     def rows(dist):
@@ -57,14 +56,12 @@
             c.start()
 
     barrier = pltpu.get_barrier_semaphore()
-    offsets = (-2, -1, 1, 2)
-    for off in offsets:
-        @pl.when((me + off >= 0) & (me + off < n))
-        def _():
-            pl.semaphore_signal(barrier, inc=1, device_id={"cp": me + off}, device_id_type=MESH)
-    behind = jnp.minimum(me, 2)
-    ahead = jnp.minimum(n - 1 - me, 2)
-    pl.semaphore_wait(barrier, behind + ahead)
+    for to, cond in ((me - 2, me >= 2), (me + 2, me + 2 < n), (partner, me >= 0)):
+        @pl.when(cond)
+        def _():
+            pl.semaphore_signal(barrier, inc=1, device_id={"cp": to}, device_id_type=MESH)
+    pl.semaphore_wait(
+        barrier, 1 + jnp.minimum(me // 2, 1) + jnp.minimum((n - 1 - me) // 2, 1))
 
     def fwd(kind, g, src_rows, dst_rows, to):
         return pltpu.make_async_remote_copy(
@@ -73,38 +70,31 @@
             device_id={"cp": to}, device_id_type=MESH,
         )
 
-    def fwd_a(g):
-        return fwd(A, g, own_rows, rows(1), partner)
+    def fwd_x(g):
+        return fwd(X, g, pl.ds((REACH - 2 * odd) * tok, tok), rows(1), partner)
 
     def fwd_b(g):
         return fwd(B, g, own_rows, rows(2), me + 2)
 
-    def fwd_c_out(g):
-        return fwd(C, g, rows(2), pl.ds(odd * 2 * tok, tok), partner)
-
-    def fwd_c_in(g):
-        return fwd(C, g, rows(2), pl.ds((1 - odd) * 2 * tok, tok), partner)
-
-    def fwd_d(g):
-        return fwd(D, g, rows(2), rows(3), diag)
-
-    has_a_out = is_even
-    has_a_in = is_odd
-    has_b_out = me + 2 < n
-    has_b_in = me >= 2
-    has_c = me >= 2
-    has_d_out = is_odd & (me >= 3) & (me + 1 < n)
-    has_d_in = is_even & (me >= 4)
+    def fwd_t(g):
+        return fwd(T, g, rows(1), rows(3), me + 2)
+
+    ahead = me + 2 < n
+    behind = me >= 2
+    x_in = is_odd | (me >= 2)
+    x_out = is_even | (me >= 3)
+    t_out = ahead & (me >= 1)
+    t_in = me >= 3
 
     for g in range(heads):
         for c in kv_loads[g]:
             c.wait()
-        @pl.when(has_b_out)
+        @pl.when(ahead)
         def _():
             fwd_b(g).start()
-        @pl.when(has_a_out)
-        def _():
-            fwd_a(g).start()
+        @pl.when(is_even)
+        def _():
+            fwd_x(g).start()
 
     for dist in range(1, REACH + 1):
         @pl.when(me < dist)
@@ -131,27 +121,26 @@
     allowed = (crossed == 0) & (key_pos <= query_pos) & (key_pos >= 0)
     bias[...] = jnp.where(allowed, 0.0, MASKED)
 
-    def relay(g):
-        @pl.when(has_b_in)
+    def relay_x(g):
+        @pl.when(behind)
         def _():
             fwd_b(g).wait_recv()
-        @pl.when(has_d_out)
-        def _():
-            fwd_d(g).start()
-        @pl.when(has_c)
-        def _():
-            fwd_c_out(g).start()
+        @pl.when(is_odd & (me >= 3))
+        def _():
+            fwd_x(g).start()
+
+    def relay_t(g):
+        @pl.when(x_in)
+        def _():
+            fwd_x(g).wait_recv()
+        @pl.when(t_out)
+        def _():
+            fwd_t(g).start()
 
     def arrive(g):
-        @pl.when(has_a_in)
-        def _():
-            fwd_a(g).wait_recv()
-        @pl.when(has_c)
-        def _():
-            fwd_c_in(g).wait_recv()
-        @pl.when(has_d_in)
-        def _():
-            fwd_d(g).wait_recv()
+        @pl.when(t_in)
+        def _():
+            fwd_t(g).wait_recv()
 
     def bwd(kind, g, src_rows, to):
         return pltpu.make_async_remote_copy(
@@ -160,17 +149,14 @@
             device_id={"cp": to}, device_id_type=MESH,
         )
 
-    def bwd_a(g):
-        return bwd(A, g, rows(1), partner)
+    def bwd_x(g):
+        return bwd(X, g, rows(1), partner)
 
     def bwd_b(g):
         return bwd(B, g, rows(2), me - 2)
 
-    def bwd_c(g):
-        return bwd(C, g, pl.ds((1 - odd) * 2 * tok, tok), partner)
-
-    def bwd_d(g):
-        return bwd(D, g, rows(3), diag)
+    def bwd_t(g):
+        return bwd(T, g, rows(3), me - 2)
 
     score_scale = 1.0 / math.sqrt(HEAD)
     exp_scale = score_scale * math.log2(math.e)
@@ -211,65 +197,68 @@
                 gq_ref[:, cols(h)] = gq_t[:, j * tok:(j + 1) * tok].T.astype(gq_ref.dtype)
         for t, grad in enumerate((grad_k * score_scale, grad_v)):
             part[g, t] = grad[:REACH * tok].astype(part.dtype)
-            mid[g, t] = grad[tok:2 * tok]
+            mid[g, t] = grad[tok:REACH * tok]
             own[g, t] = grad[REACH * tok:]
 
-    def give_back(g):
-        @pl.when(has_d_in)
-        def _():
-            bwd_d(g).start()
-        @pl.when(has_c)
-        def _():
-            bwd_c(g).start()
-        @pl.when(has_a_in)
-        def _():
-            bwd_a(g).start()
-
-    def collect(g):
-        @pl.when(has_c)
-        def _():
-            bwd_c(g).wait_recv()
-            mid[g] = mid[g] + back[C, g].astype(jnp.float32)
-        @pl.when(has_d_out)
-        def _():
-            bwd_d(g).wait_recv()
-            mid[g] = mid[g] + back[D, g].astype(jnp.float32)
-        @pl.when(has_b_in)
-        def _():
-            part[g, :, tok:2 * tok] = mid[g].astype(part.dtype)
+    def back_t(g):
+        @pl.when(t_in)
+        def _():
+            bwd_t(g).start()
+
+    def back_x(g):
+        @pl.when(t_out)
+        def _():
+            bwd_t(g).wait_recv()
+            part[g, :, 2 * tok:] = (
+                mid[g, :, tok:] + back[T, g].astype(jnp.float32)).astype(part.dtype)
+        @pl.when(x_in)
+        def _():
+            bwd_x(g).start()
+
+    def back_b(g):
+        @pl.when(x_out)
+        def _():
+            bwd_x(g).wait_recv()
+        @pl.when(is_even)
+        def _():
+            own[g] = own[g] + back[X, g].astype(jnp.float32)
+        @pl.when(is_odd & (me >= 3))
+        def _():
+            part[g, :, tok:2 * tok] = (
+                mid[g, :, :tok] + back[X, g].astype(jnp.float32)).astype(part.dtype)
+        @pl.when(behind)
+        def _():
             bwd_b(g).start()
 
     def finish(g):
-        @pl.when(has_a_out)
-        def _():
-            bwd_a(g).wait_recv()
-            own[g] = own[g] + back[A, g].astype(jnp.float32)
-        @pl.when(has_b_out)
+        @pl.when(ahead)
         def _():
             bwd_b(g).wait_recv()
             own[g] = own[g] + back[B, g].astype(jnp.float32)
         gk_ref[:, cols(g)] = own[g, 0].astype(gk_ref.dtype)
         gv_ref[:, cols(g)] = own[g, 1].astype(gv_ref.dtype)
 
-    relay(0)
-    for g in range(heads):
-        if g + 1 < heads:
-            relay(g + 1)
-        arrive(g)
-        compute(g)
-        give_back(g)
-        if g >= 1:
-            collect(g - 1)
-        if g >= 2:
-            finish(g - 2)
-    collect(heads - 1)
-    for g in range(max(heads - 2, 0), heads):
-        finish(g)
+    relay_x(0)
+    if heads > 1:
+        relay_x(1)
+    relay_t(0)
+    for g in range(heads + REACH):
+        if g < heads:
+            if g + 2 < heads:
+                relay_x(g + 2)
+            if g + 1 < heads:
+                relay_t(g + 1)
+            arrive(g)
+            compute(g)
+            back_t(g)
+        for lag, stage in enumerate((back_x, back_b, finish)):
+            if 0 <= g - 1 - lag < heads:
+                stage(g - 1 - lag)
 
     for g in range(heads):
         for cond, copies in (
-            (has_a_out, (fwd_a,)), (has_b_out, (fwd_b,)), (has_c, (fwd_c_out, bwd_c)),
-            (has_d_out, (fwd_d,)), (has_a_in, (bwd_a,)), (has_b_in, (bwd_b,)), (has_d_in, (bwd_d,)),
+            (ahead, (fwd_b,)), (x_out, (fwd_x,)), (t_out, (fwd_t,)),
+            (behind, (bwd_b,)), (x_in, (bwd_x,)), (t_in, (bwd_t,)),
         ):
             @pl.when(cond)
             def _():
@@ -317,18 +306,18 @@
             pltpu.VMEM((q_heads, tok, HEAD), bf16),
             pltpu.VMEM((q_heads, tok, HEAD), bf16),
             pltpu.VMEM((heads, 2, tok, HEAD), f32),
-            pltpu.VMEM((heads, 2, tok, HEAD), f32),
+            pltpu.VMEM((heads, 2, 2 * tok, HEAD), f32),
             pltpu.VMEM((heads, 2, REACH * tok, HEAD), bf16),
-            pltpu.VMEM((4, heads, 2, tok, HEAD), bf16),
+            pltpu.VMEM((3, heads, 2, tok, HEAD), bf16),
             pltpu.VMEM((window, tok), f32),
             pltpu.SMEM(doc_lengths.shape, jnp.int32),
             dma(()),
             dma((heads, 2)),
             dma((2, q_heads)),
-            dma((4, heads)),
-            dma((4, heads)),
-            dma((4, heads)),
-            dma((4, heads)),
+            dma((3, heads)),
+            dma((3, heads)),
+            dma((3, heads)),
+            dma((3, heads)),
         ],
         compiler_params=pltpu.CompilerParams(
             collective_id=0, has_side_effects=True, vmem_limit_bytes=24 * 2**20),

time: 39.4 us -> 40.3 us (1.023); the launches traced: 38.7 us -> 40.1 us
  Pallas kernels: 38 us -> 39.5 us
    pallas_call x1, Pallas kernels: 36.9 us -> 38.4 us  [shards(): pl.pallas_call(functools.partial(kernel, n, doc_lengths.shape[0]), out_sh...]
where the time goes in v3:
time: 40.3 us; the launch traced here: 40.1 us
  Pallas kernels  39.5 us (98%)
  between operations  0.64 us (2%)
    pallas_call x1, Pallas kernels, shards(): pl.pallas_call(functools.partial(kernel, n, doc_lengths.shape[0]), out_sh...  38.4 us
    pallas_call x1, Pallas kernels, shards(): pl.pallas_call(put_out, out_shape=[jax.ShapeDtypeStruct(x.shape, x.dtype)...  1.08 us

profile of v3, /device:TPU:0, one launch (start us, length us, event | category | flops | bytes accessed | tf_op | source)
XLA Modules:
  0.0 40.1 jit_solution(9004319670225615866)
XLA Ops:
  0.6 38.4 %attend.1 = (bf16[128,2048]{1,0:T(8,128)(2,1)S(1)}, bf16[128,2048]{1,0:T(8,128)(2,1)S(1)}, bf16[128,512]{1,0:T(8,128)(2,1)S(1)}, bf16[128,512]{1,0:T(8,128)(2,1)S(1)}) custom-call(s32[4]{0:T(128)} %doc_hbm.1, bf16[128,2048]{1,0:T(8,128)(2,1)} %q_hbm.1, bf16[128,512]{1,0:T(8,128)(2,1)} %k_hbm.1, bf16[128,512]{1,0:T(8,128)(2,1)} %v_hbm.1, bf16[128,2048]{1,0:T(8,128)(2,1)} %do_hbm.1), custom_call_target="tpu_custom_call" | custom-call | tf_op jit(solution)/shard_map/attend/pallas_call | solution.py:294
  39.0 1.1 %put_out.1 = (bf16[128,2048]{1,0:T(8,128)(2,1)}, bf16[128,2048]{1,0:T(8,128)(2,1)}, bf16[128,512]{1,0:T(8,128)(2,1)}, bf16[128,512]{1,0:T(8,128)(2,1)}) custom-call(bf16[128,2048]{1,0:T(8,128)(2,1)S(1)} %get-tuple-element.8.refs_0_, bf16[128,2048]{1,0:T(8,128)(2,1)S(1)} %get-tuple-element.9.refs_1_, bf16[128,512]{1,0:T(8,128)(2,1)S(1)} %get-tuple-element.10.refs_2_, ...), custom_call_target="tpu_custom_call" | custom-call | tf_op jit(solution)/shard_map/put_out/pallas_call | solution.py:326

commit v4 on v3

--- a/solution.py
+++ b/solution.py
@@ -204,6 +204,9 @@
         @pl.when(t_in)
         def _():
             bwd_t(g).start()
+        @pl.when(is_even & behind)
+        def _():
+            bwd_b(g).start()
 
     def back_x(g):
         @pl.when(t_out)
@@ -216,21 +219,18 @@
             bwd_x(g).start()
 
     def back_b(g):
-        @pl.when(x_out)
+        @pl.when(is_odd & (me >= 3))
         def _():
             bwd_x(g).wait_recv()
-        @pl.when(is_even)
-        def _():
-            own[g] = own[g] + back[X, g].astype(jnp.float32)
-        @pl.when(is_odd & (me >= 3))
-        def _():
             part[g, :, tok:2 * tok] = (
                 mid[g, :, :tok] + back[X, g].astype(jnp.float32)).astype(part.dtype)
-        @pl.when(behind)
-        def _():
             bwd_b(g).start()
 
     def finish(g):
+        @pl.when(is_even)
+        def _():
+            bwd_x(g).wait_recv()
+            own[g] = own[g] + back[X, g].astype(jnp.float32)
         @pl.when(ahead)
         def _():
             bwd_b(g).wait_recv()

time: 40.3 us -> 37.4 us (0.928)
  the two profiles are of different devices: /device:TPU:0 before, /device:TPU:2 now
where the time goes in v4:
time: 37.4 us; the launch traced here: 37.3 us
  Pallas kernels  36.6 us (98%)
  between operations  0.64 us (2%)
    pallas_call x1, Pallas kernels, shards(): pl.pallas_call(functools.partial(kernel, n, doc_lengths.shape[0]), out_sh...  35.5 us
    pallas_call x1, Pallas kernels, shards(): pl.pallas_call(put_out, out_shape=[jax.ShapeDtypeStruct(x.shape, x.dtype)...  1.08 us

profile of v4, /device:TPU:2, one launch (start us, length us, event | category | flops | bytes accessed | tf_op | source)
XLA Modules:
  0.0 37.3 jit_solution(2734564178575481527)
XLA Ops:
  0.6 35.5 %attend.1 = (bf16[128,2048]{1,0:T(8,128)(2,1)S(1)}, bf16[128,2048]{1,0:T(8,128)(2,1)S(1)}, bf16[128,512]{1,0:T(8,128)(2,1)S(1)}, bf16[128,512]{1,0:T(8,128)(2,1)S(1)}) custom-call(s32[4]{0:T(128)} %doc_hbm.1, bf16[128,2048]{1,0:T(8,128)(2,1)} %q_hbm.1, bf16[128,512]{1,0:T(8,128)(2,1)} %k_hbm.1, bf16[128,512]{1,0:T(8,128)(2,1)} %v_hbm.1, bf16[128,2048]{1,0:T(8,128)(2,1)} %do_hbm.1), custom_call_target="tpu_custom_call" | custom-call | tf_op jit(solution)/shard_map/attend/pallas_call | solution.py:294
  36.2 1.1 %put_out.1 = (bf16[128,2048]{1,0:T(8,128)(2,1)}, bf16[128,2048]{1,0:T(8,128)(2,1)}, bf16[128,512]{1,0:T(8,128)(2,1)}, bf16[128,512]{1,0:T(8,128)(2,1)}) custom-call(bf16[128,2048]{1,0:T(8,128)(2,1)S(1)} %get-tuple-element.8.refs_0_, bf16[128,2048]{1,0:T(8,128)(2,1)S(1)} %get-tuple-element.9.refs_1_, bf16[128,512]{1,0:T(8,128)(2,1)S(1)} %get-tuple-element.10.refs_2_, ...), custom_call_target="tpu_custom_call" | custom-call | tf_op jit(solution)/shard_map/put_out/pallas_call | solution.py:326
